TPU v7x, 512 devices: a whole 4x8x8 slice. The times are simulated.
512 devices in a mesh: elem: 128 (over z, x_lo, y), chan: 4 (over x_hi, core).
Axes of the slice: x: 4 (x_hi: 2, x_lo: 2; x = x_hi * 2 + x_lo), y: 8, z: 8, core: 2. Of those that a mesh axis runs over, the one named last changes fastest.
Arguments:
- voltages: bfloat16 [2, 16384, 19584], P(None, ('elem', 'chan')), may hold values from -6 to 6
- delays: int32 [16384], P(('elem', 'chan')), may hold values from 0 to 127
- prototype: bfloat16 [16, 1024], replicated, may hold values from -1.5 to 1.5
- subband_map: int32 [16], replicated, may hold values from 0 to 1023, as said below
- beam_weights: bfloat16 [512, 2, 16, 16384], P('elem', None, 'chan'), may hold values from -0.1875 to 0.1875
Outputs:
- element_power: bfloat16 [16384, 1024], P(('elem', 'chan'))
- beam_voltages: float32 [2, 64, 512], P(None, 'chan', 'elem')
Inputs may be any that keep to these rules, and one draw needn't show every extreme that they name: `subband_map`: distinct channel numbers.
All inputs are finite; a program needn't handle non-finite values.
Results may differ from a plain program's by a relative error of at most 0.007.
Values may be sent and summed in bfloat16 or wider, within the bound.
A program may use at most 128 MiB of HBM per device.

v0:
```python
import math

import jax
import jax.numpy as jnp
from jax import lax
from jax.sharding import Mesh
from jax.sharding import PartitionSpec as P

FRAMES = 4
SUB_C = 4
ELEM = ("elem_0", "elem_1", "elem_2")
ELEM_CHAN = ("elem_0", "elem_1", "elem_2", "chan")


def in_order(parts, dim):
    parts = jnp.moveaxis(parts, 0, dim)
    dims = parts.shape
    return parts.reshape(*dims[:dim], dims[dim] * dims[dim + 1], *dims[dim + 2 :])


def all_blocks(array, axes, turns):
    parts = array[None]
    for k in turns:
        parts = lax.all_gather(parts, axes[k], axis=0, tiled=True)
    held = [lax.axis_size(axes[k]) for k in reversed(turns)]
    parts = parts.reshape(*held, *array.shape)
    turned = sorted(range(len(turns)), key=lambda place: turns[len(turns) - 1 - place])
    return parts.transpose(*turned, *range(len(turns), parts.ndim)).reshape(-1, *array.shape)


def gather_axes(array, axes, turns, dim):
    return in_order(all_blocks(array, axes, turns), dim)


def filtered(voltages, delays, prototype):
    tap_count, chan_count = prototype.shape
    blocks = FRAMES + tap_count - 1
    window_len = blocks * chan_count

    def window(samples, offset):
        return lax.dynamic_slice_in_dim(samples, offset, window_len, 0)

    segments = jax.vmap(jax.vmap(window, in_axes=(0, 0)), in_axes=(0, None))(voltages, delays)
    segments = segments.reshape(voltages.shape[0], voltages.shape[1], blocks, chan_count)
    coeffs = prototype.astype(jnp.float32)
    running = jnp.zeros((voltages.shape[0], voltages.shape[1], FRAMES, chan_count), jnp.float32)
    for tap_index in range(tap_count):
        running = running + coeffs[tap_index] * segments[
            :, :, tap_index : tap_index + FRAMES, :
        ].astype(jnp.float32)
    return running.astype(jnp.bfloat16)


def spectra(filtered_wave):
    part_count, elem_count, frame_count, chan_count = filtered_wave.shape
    counter = jnp.arange(chan_count, dtype=jnp.int32)
    residue = counter[:, None] * counter[None, :] % chan_count
    radians = residue.astype(jnp.float32) * (2.0 * math.pi / chan_count)
    factor = 1.0 / math.sqrt(chan_count)
    basis = jnp.concatenate([jnp.cos(radians) * factor, jnp.sin(radians) * factor], axis=1)
    basis_high = basis.astype(jnp.bfloat16)
    basis_low = (basis - basis_high.astype(jnp.float32)).astype(jnp.bfloat16)
    flattened = filtered_wave.reshape(part_count * elem_count * frame_count, chan_count)
    product = jnp.dot(flattened, basis_high, preferred_element_type=jnp.float32)
    product = product + jnp.dot(flattened, basis_low, preferred_element_type=jnp.float32)
    product = product.reshape(part_count, elem_count, frame_count, 2, chan_count)
    spec_real = product[0, :, :, 0] + product[1, :, :, 1]
    spec_imag = product[1, :, :, 0] - product[0, :, :, 1]
    return (spec_real, spec_imag)


def beam_terms(spectra_part, weight_part):
    weight_real = weight_part[:, 0]
    weight_imag = weight_part[:, 1]

    def contract(spectral, weighting):
        return jnp.einsum("sfe,bse->sfb", spectral, weighting, preferred_element_type=jnp.float32)

    out_real = contract(spectra_part[0], weight_real) - contract(spectra_part[1], weight_imag)
    out_imag = contract(spectra_part[1], weight_real) + contract(spectra_part[0], weight_imag)
    return jnp.stack([out_real, out_imag])


def on_device(voltages, delays, prototype, subband_map, beam_weights):
    filtered_wave = filtered(voltages, delays, prototype)
    spec_real, spec_imag = spectra(filtered_wave)
    element_power = jnp.mean(spec_real * spec_real + spec_imag * spec_imag, axis=1).astype(
        jnp.bfloat16
    )
    picked = jnp.stack([spec_real[:, :, subband_map], spec_imag[:, :, subband_map]]).astype(
        jnp.bfloat16
    )
    picked = jnp.transpose(picked, (0, 3, 2, 1))
    turned = lax.all_to_all(picked, "chan", split_axis=1, concat_axis=3, tiled=True)
    local_beams = beam_weights.shape[0]
    summed = beam_terms(gather_axes(turned, ELEM, (1, 0, 2), 3), beam_weights)
    beam_voltages = summed.reshape(2, SUB_C * FRAMES, local_beams)
    return (element_power, beam_voltages)


def solution(mesh):
    finer = Mesh(
        mesh.devices.reshape(8, 2, 8, mesh.shape["chan"]), ("elem_0", "elem_1", "elem_2", "chan")
    )
    placed = (P(None, ELEM_CHAN, None), P(ELEM_CHAN), P(), P(), P(ELEM, None, "chan", None))
    return jax.shard_map(
        on_device,
        mesh=finer,
        in_specs=placed,
        out_specs=(P(ELEM_CHAN, None), P(None, "chan", ELEM)),
        check_vma=False,
    )
```

profile of v0, /device:TPU:1, one launch (start us, length us, event | category | flops | bytes accessed | tf_op | source)
XLA Modules:
  0.0 258.3 jit_solution(16402044286607184922)
XLA Ops:
  7.2 17.8 %sine_multiply_fusion = (f32[1024,1024]{1,0:T(8,128)}, f32[1024,1024]{1,0:T(8,128)}) fusion(), kind=kLoop, calls=%fused_computation.14 | loop fusion | flops 16777216 | bytes 8388608 | tf_op jit(solution)/shard_map/mul | solution.py:60
  25.1 1.9 copy.40
  27.1 88.3 %while.1 = (s32[]{:T(128)}, bf16[2,32,19584]{2,0,1:T(2,128)(2,1)S(1)}, s32[32,2]{0,1:T(2,128)S(1)}, bf16[32,2,19456]{2,1,0:T(2,128)(2,1)}, s32[]{:T(128)}) while((s32[]{:T(128)}, bf16[2,32,19584]{2,0,1:T(2,128)(2,1)S(1)}, s32[32,2]{0,1:T(2,128)S(1)}, bf16[32,2,19456]{2,1,0:T(2,128)(2,1)}, s32[]{:T(128)}) %tuple.51), condition=%wide.while_cond, body=%wide.while_body.sunk | while | flops 2 | bytes 157281 | solution.py:41
  27.8 2.1 bitcast_dynamic-update-slice_fusion.2
  30.5 2.1 bitcast_dynamic-update-slice_fusion.2
  33.3 2.1 bitcast_dynamic-update-slice_fusion.2
  36.0 2.1 bitcast_dynamic-update-slice_fusion.2
  38.8 2.1 bitcast_dynamic-update-slice_fusion.2
  41.5 2.1 bitcast_dynamic-update-slice_fusion.2
  44.3 2.1 bitcast_dynamic-update-slice_fusion.2
  47.1 2.1 bitcast_dynamic-update-slice_fusion.2
  49.8 2.1 bitcast_dynamic-update-slice_fusion.2
  52.6 2.1 bitcast_dynamic-update-slice_fusion.2
  55.3 2.1 bitcast_dynamic-update-slice_fusion.2
  58.1 2.1 bitcast_dynamic-update-slice_fusion.2
  60.8 2.1 bitcast_dynamic-update-slice_fusion.2
  63.6 2.1 bitcast_dynamic-update-slice_fusion.2
  66.4 2.1 bitcast_dynamic-update-slice_fusion.2
  69.1 2.1 bitcast_dynamic-update-slice_fusion.2
  71.9 2.1 bitcast_dynamic-update-slice_fusion.2
  74.6 2.1 bitcast_dynamic-update-slice_fusion.2
  77.4 2.1 bitcast_dynamic-update-slice_fusion.2
  80.1 2.1 bitcast_dynamic-update-slice_fusion.2
  82.9 2.1 bitcast_dynamic-update-slice_fusion.2
  85.7 2.1 bitcast_dynamic-update-slice_fusion.2
  88.4 2.1 bitcast_dynamic-update-slice_fusion.2
  91.2 2.1 bitcast_dynamic-update-slice_fusion.2
  93.9 2.1 bitcast_dynamic-update-slice_fusion.2
  96.7 2.1 bitcast_dynamic-update-slice_fusion.2
  99.5 2.1 bitcast_dynamic-update-slice_fusion.2
  102.2 2.1 bitcast_dynamic-update-slice_fusion.2
  105.0 2.1 bitcast_dynamic-update-slice_fusion.2
  107.7 2.1 bitcast_dynamic-update-slice_fusion.2
  110.5 2.1 bitcast_dynamic-update-slice_fusion.2
  113.2 2.1 bitcast_dynamic-update-slice_fusion.2
  115.3 3.6 %copy.41 = bf16[2,32,19456]{2,1,0:T(8,128)(2,1)} copy(bf16[2,32,19456]{2,0,1:T(2,128)(2,1)} %bitcast.82) | data formatting | bytes 4980736 | tf_op jit(solution)/shard_map/vmap(vmap())/gather | solution.py:41
  119.0 3.3 %reshape.48 = bf16[2,32,19,1024]{3,2,1,0:T(8,128)(2,1)S(1)} reshape(bf16[2,32,19456]{2,1,0:T(8,128)(2,1)} %copy.41) | data formatting | bytes 4980736 | tf_op jit(solution)/shard_map/reshape | solution.py:44
  122.3 5.1 %add_convert_fusion = bf16[2,32,4,1024]{3,2,1,0:T(4,128)(2,1)} fusion(bf16[2,32,19,1024]{3,2,1,0:T(8,128)(2,1)S(1)} %reshape.48, f32[1024]{0:T(1024)S(1)} %bitcast.102, f32[1024]{0:T(1024)S(1)} %bitcast.101, f32[1024]{0:T(1024)S(1)} %bitcast.100, f32[1024]{0:T(1024)S(1)} %bitcast.99, f32[1024]{0:T(1024)S(1)} %bitcast.98, f32[1024]{0:T(1024)S(1)} %bitcast.97, ...), kind=kLoop, calls=%fused_computation.26 | loop fusion | flops 12582912 | bytes 8978432 | tf_op jit(solution)/shard_map/convert_element_type | solution.py:51
  127.4 1.2 reshape.49
  128.6 4.8 %fusion.1 = f32[256,2048]{1,0:T(8,128)S(1)} fusion(bf16[256,1024]{1,0:T(8,128)(2,1)S(1)} %reshape.49, f32[1024,1024]{1,0:T(8,128)} %get-tuple-element.61, f32[1024,1024]{1,0:T(8,128)} %get-tuple-element.62), kind=kOutput, calls=%fused_computation.10 | convolution fusion | flops 1082130432 | bytes 11010048 | tf_op jit(solution)/shard_map/dot_general | solution.py:64
  133.5 1.0 copy-done.1
  134.5 1.3 fusion.10
  135.8 2.8 %reshape.50 = f32[2,32,4,2,1024]{4,3,2,1,0:T(2,128)} reshape(f32[256,2048]{1,0:T(8,128)S(1)} %fusion.10) | data formatting | bytes 4194304 | tf_op jit(solution)/shard_map/reshape | solution.py:66
  138.6 5.4 %fusion.17 = (f32[1,32,4,1,1024]{4,3,2,1,0:T(1,128)S(1)}, f32[1,32,4,1,1024]{4,3,2,1,0:T(1,128)S(1)}, f32[1,32,4,1,1024]{4,3,2,1,0:T(1,128)}, f32[1,32,4,1,1024]{4,3,2,1,0:T(1,128)}) fusion(f32[2,32,4,2,1024]{4,3,2,1,0:T(2,128)} %reshape.50), kind=kLoop, calls=%fused_computation.44 | loop fusion | bytes 4194304 | tf_op jit(solution)/shard_map/slice | solution.py:68
  144.0 2.7 %copy.58 = f32[1,32,4,1,1024]{1,2,4,3,0:T(4,128)S(1)} copy(f32[1,32,4,1,1024]{4,3,2,1,0:T(1,128)} %get-tuple-element.40) | data formatting | bytes 1048576
  146.7 3.3 %copy.59 = f32[1,32,4,1,1024]{1,2,4,3,0:T(4,128)} copy(f32[1,32,4,1,1024]{4,3,2,1,0:T(1,128)} %get-tuple-element.39) | data formatting | bytes 1048576
  150.1 2.4 copy.60
  152.5 2.4 copy.61
  154.9 5.7 %add_reduce_fusion = (f32[32,1024]{0,1:T(8,128)S(1)}, bf16[32,4,1024]{0,1,2:T(4,128)(2,1)}, bf16[32,4,1024]{0,1,2:T(4,128)(2,1)}) fusion(f32[1,32,4,1,1024]{1,2,4,3,0:T(4,128)S(1)} %copy.58, f32[1,32,4,1,1024]{1,2,4,3,0:T(4,128)} %copy.59, f32[1,32,4,1,1024]{1,2,4,3,0:T(4,128)} %copy.60, f32[1,32,4,1,1024]{1,2,4,3,0:T(4,128)} %copy.61), kind=kLoop, calls=%fused_computation.21 | loop fusion | flops 1015808 | bytes 2752512 | tf_op jit(solution)/shard_map/reduce_sum | solution.py:87
  160.6 1.8 gather_fusion.1
  162.4 1.8 gather_fusion
  164.2 0.7 reshape.92
  164.9 10.0 %all-to-all-start = ((bf16[4,2,512]{2,1,0:T(2,128)(2,1)}), bf16[4,2,512]{2,1,0:T(2,128)(2,1)S(1)}, u32[]{:S(2)}, u32[]{:S(2)}) async-start(bf16[4,2,512]{2,1,0:T(2,128)(2,1)} %reshape.92), calls=%async_computation | async-start | bytes 16384 | tf_op jit(solution)/shard_map/all_to_all | solution.py:94
  175.0 0.8 copy.55
  175.8 3.8 %all-to-all-done = bf16[4,2,512]{2,1,0:T(2,128)(2,1)S(1)} async-done(((bf16[4,2,512]{2,1,0:T(2,128)(2,1)}), bf16[4,2,512]{2,1,0:T(2,128)(2,1)S(1)}, u32[]{:S(2)}, u32[]{:S(2)}) %all-to-all-start) | async-done | bytes 8224 | tf_op jit(solution)/shard_map/all_to_all | solution.py:94
  179.8 3.2 %all_gather.9 = bf16[2,2,4,4,128]{4,3,2,1,0:T(4,128)(2,1)S(1)} all-gather(bf16[1,2,4,4,128]{4,3,2,1,0:T(4,128)(2,1)S(1)} %broadcast_in_dim.14), channel_id=1, replica_groups=mesh['elem_0'=8,'elem_1'=2,'elem_2'=8,'chan'=4] {'elem_1'}, dimensions={0}, use_global_device_ids=true | all-gather | bytes 24576 | tf_op jit(solution)/shard_map/all_gather | solution.py:24
  183.0 22.3 %all_gather.10 = bf16[16,2,4,4,128]{4,3,2,1,0:T(4,128)(2,1)} all-gather(bf16[2,2,4,4,128]{4,3,2,1,0:T(4,128)(2,1)S(1)} %all_gather.9), channel_id=1, replica_groups=mesh['elem_0'=8,'elem_1'=2,'elem_2'=8,'chan'=4] {'elem_0'}, dimensions={0}, use_global_device_ids=true | all-gather | bytes 147456 | tf_op jit(solution)/shard_map/all_gather | solution.py:24
  205.4 1.6 fusion.18
  206.9 37.9 %all-gather.2.cloned.1.call-done = bf16[128,2,4,4,128]{4,3,2,1,0:T(4,128)(2,1)} async-done(((bf16[16,2,4,4,128]{4,3,2,1,0:T(4,128)(2,1)}), bf16[128,2,4,4,128]{4,3,2,1,0:T(4,128)(2,1)}) %all-gather.2.cloned.1.call-update) | async-done | bytes 1048592 | tf_op jit(solution)/shard_map/all_gather | solution.py:24
  244.8 1.6 copy.49
  247.4 0.8 fusion.12
  248.2 0.8 fusion.11
  249.0 0.8 convolution_subtract_fusion
  250.0 0.8 convolution_add_fusion
  (97 shorter events, 22.8 us)
Async XLA Ops:
  7.2 17.8 %copy-start.3 = (bf16[16,1024]{1,0:T(8,128)(2,1)S(1)}, bf16[16,1024]{1,0:T(8,128)(2,1)}, u32[]{:S(2)}) copy-start(bf16[16,1024]{1,0:T(8,128)(2,1)} %param.7) | copy-start | bytes 98308
  7.2 17.9 %copy-start.2 = (bf16[2,32,19584]{2,1,0:T(8,128)(2,1)S(1)}, bf16[2,32,19584]{2,1,0:T(8,128)(2,1)}, u32[]{:S(2)}) copy-start(bf16[2,32,19584]{2,1,0:T(8,128)(2,1)} %param.5) | copy-start | bytes 7520260
  25.0 2.0 copy-start.4
  128.6 4.9 %copy-start = (f32[1024,1024]{1,0:T(8,128)S(1)}, f32[1024,1024]{1,0:T(8,128)}, u32[]{:S(2)}) copy-start(f32[1024,1024]{1,0:T(8,128)} %get-tuple-element.61) | copy-start | bytes 12582916
  128.6 5.9 %copy-start.1 = (f32[1024,1024]{1,0:T(8,128)S(1)}, f32[1024,1024]{1,0:T(8,128)}, u32[]{:S(2)}) copy-start(f32[1024,1024]{1,0:T(8,128)} %get-tuple-element.62) | copy-start | bytes 12582916
  146.7 8.2 %copy-start.5 = (s32[16]{0:T(128)S(1)}, s32[16]{0:T(128)}, u32[]{:S(2)}) copy-start(s32[16]{0:T(128)} %param.8) | copy-start | bytes 196
  164.9 14.7 %all-to-all-start = ((bf16[4,2,512]{2,1,0:T(2,128)(2,1)}), bf16[4,2,512]{2,1,0:T(2,128)(2,1)S(1)}, u32[]{:S(2)}, u32[]{:S(2)}) async-start(bf16[4,2,512]{2,1,0:T(2,128)(2,1)} %reshape.92), calls=%async_computation | async-start | bytes 16384 | tf_op jit(solution)/shard_map/all_to_all | solution.py:94
  175.0 69.9 %all-gather.2.cloned.1.call-start = ((), (), s32[]{:S(2)}) async-start(), calls=%async_computation.1 | async-start | bytes 1179648 | tf_op jit(solution)/shard_map/all_gather | solution.py:24
Sparse Core Ops, SparseCore 0:
  205.5 39.3 all-gather.1
where the time goes:
time: 263 us; the launch traced here: 258 us
  local copies, waits for them, and re-layouts  128 us (49%)
  waiting for transfers between devices  41.7 us (16%)
  other arithmetic  29.3 us (11%)
  blocking collectives  25.5 us (10%)
  between operations  14.3 us (5%)
  starting transfers between devices  10 us (4%)
  matrix products  9.47 us (4%)
    gather x96, local copies, waits for them, and re-layouts  88.2 us
    all_gather x1, waiting for transfers between devices, all_blocks(): parts = lax.all_gather(parts, axes[k], axis=0, tiled=True)  37.9 us
    all_gather x2, blocking collectives, all_blocks(): parts = lax.all_gather(parts, axes[k], axis=0, tiled=True)  25.5 us
    mul x1, other arithmetic, spectra(): jnp.sin(radians) * factor  17.8 us
    unnamed x21, local copies, waits for them, and re-layouts  15.4 us
    all_to_all x1, starting transfers between devices, on_device(): lax.all_to_all(picked, 'chan', split_axis=1, concat_axis=3, tiled=True)  10 us
    reduce_sum x1, other arithmetic, on_device(): jnp.mean(spec_real * spec_real + spec_imag * spec_imag, axis=1)  5.69 us
    slice x1, local copies, waits for them, and re-layouts, spectra(): spec_imag = product[1, :, :, 0] - product[0, :, :, 1]  5.37 us
  transfers between devices with their start and end apart: 2, of which 2 were waited for; matrix products, arithmetic and copies ran while one was open for 1% of the time, Pallas kernels for 0%

commit v1 on v0

v1 whole, which is shorter than its diff:
```python
import functools
import math

import numpy as np
import jax
import jax.numpy as jnp
from jax import lax
from jax.experimental import pallas as pl
from jax.experimental.pallas import tpu as pltpu
from jax.sharding import Mesh
from jax.sharding import PartitionSpec as P

MESH = pl.DeviceIdType.MESH
CH, TAPS, FRAMES, E_DEV = 1024, 16, 4, 32
BLOCKS = FRAMES + TAPS - 1
SAMP = 19584
RING = 8
LINE = 8
PAD = 40
ORDER = (0, 1, 7, 2, 6, 3, 5, 4)
F32, BF16 = jnp.float32, jnp.bfloat16


def dft_blocks():
    k1 = np.arange(8)[:, None, None]
    p2 = np.arange(128)[None, :, None]
    k2 = np.arange(128)[None, None, :]
    angle = ((p2 * (k1 + 8 * k2)) % CH) * (2.0 * np.pi / CH)
    c, s = np.cos(angle), np.sin(angle)
    top = np.concatenate([c, -s], axis=2)
    low = np.concatenate([s, c], axis=2)
    return np.concatenate([top, low], axis=1).astype(jnp.bfloat16)


def iota(shape, dim):
    return lax.broadcasted_iota(jnp.int32, shape, dim)


def cos_turns(u):
    h = (u - jnp.round(u)) * math.pi
    q = h * h
    s = h * (1.0 + q * (-1.0 / 6 + q * (1.0 / 120 + q * (-1.0 / 5040 + q * (1.0 / 362880 - q * (1.0 / 39916800))))))
    return 1.0 - 2.0 * s * s


def nt_dot(a, b):
    return lax.dot_general(a, b, (((1,), (1,)), ((), ())), preferred_element_type=F32)


def rotated_taps(delay_s, proto_v, taps_a, taps_b, coef):
    taps = proto_v[...].astype(F32)
    for j in range(8):
        block = taps[:, 128 * j : 128 * j + 128]
        taps_a[pl.ds(j, TAPS, stride=8), :] = block
        taps_b[pl.ds((j + 1) % 8, TAPS, stride=8), :] = block
    lane = iota((128, 128), 1)

    def one(n, carry):
        d = delay_s[n]
        mixed = jnp.where(lane < 128 - d, taps_a[...], taps_b[...])
        coef[pl.ds(n, 128, stride=PAD), :] = pltpu.roll(mixed, d, 1)
        return carry

    lax.fori_loop(0, E_DEV, one, 0)


def delay_column(delay_s, column):
    row = iota((E_DEV, 128), 0)
    value = jnp.zeros((E_DEV, 128), jnp.int32)
    for n in range(E_DEV):
        value = jnp.where(row == n, delay_s[n], value)
    column[...] = value


def channel_rows(map_s, rows):
    row = iota((rows, 128), 0)
    which = ((row // 8) % 4) * 4 + row % 4
    value = jnp.zeros((rows, 128), jnp.int32)
    for s in range(16):
        value = jnp.where(which == s, map_s[s], value)
    return value.astype(F32)


def chosen_basis(map_s, basis):
    chan = channel_rows(map_s, 64) * (1.0 / CH)
    row = iota((64, 128), 0)
    swapped, second = row // 32, (row // 4) % 2
    zero = jnp.zeros((64, 128), F32)
    first_half = jnp.where(swapped == 0, jnp.where(second == 0, zero, 0.25), jnp.where(second == 0, -0.25, zero))
    last_half = jnp.where(swapped == 0, jnp.where(second == 0, -0.25, zero), jnp.where(second == 0, 0.5 + zero, -0.25))
    lane = iota((64, 128), 1)
    for j in range(8):
        turns = chan * (lane + 128 * j).astype(F32)
        basis[:, 128 * j : 128 * j + 128] = cos_turns(turns + first_half).astype(BF16)
        basis[:, CH + 128 * j : CH + 128 * j + 128] = cos_turns(turns + last_half).astype(BF16)


def filter_block(part, g, j, special, volt, coef, column, wave):
    rows = slice(16 * g, 16 * g + 16)

    def samples(b):
        start = b * CH + 128 * j
        if not isinstance(j, int):
            start = pl.multiple_of(start, 128)
        return volt[part, rows, pl.ds(start, 128)].astype(F32)

    sums = [None] * FRAMES
    if special:
        late = iota((16, 128), 1) < column[rows, :]
        following = samples(0)
    taps = {}
    for b in range(BLOCKS):
        if special:
            now = following
            following = samples(b + 1)
            value = jnp.where(late, following, now)
        else:
            value = samples(b)
        if b < TAPS:
            start = (b * 8 + j) * PAD + 16 * g
            if not isinstance(j, int):
                start = pl.multiple_of(start, 8)
            taps[b] = coef[pl.ds(start, 16), :]
        for f in range(FRAMES):
            t = b - f
            if 0 <= t < TAPS:
                term = taps[t] * value
                sums[f] = term if sums[f] is None else sums[f] + term
    column_start = part * CH + 128 * j
    if not isinstance(j, int):
        column_start = pl.multiple_of(column_start, 128)
    for f in range(FRAMES):
        wave[pl.ds(f * E_DEV + 16 * g, 16), pl.ds(column_start, 128)] = sums[f].astype(BF16)


def filter_chunk(part, g, volt, coef, column, wave):
    filter_block(part, g, 0, True, volt, coef, column, wave)

    def one(j, carry):
        filter_block(part, g, j, False, volt, coef, column, wave)
        return carry

    lax.fori_loop(1, 8, one, 0)


def chosen_spectra(delay_s, map_s, basis, wave, chosen):
    both = nt_dot(basis[...], wave[...])
    lane = iota((32, 128), 1) % E_DEV
    delay = jnp.zeros((32, 128), jnp.int32)
    for n in range(E_DEV):
        delay = jnp.where(lane == n, delay_s[n], delay)
    turns = channel_rows(map_s, 32) * delay.astype(F32) * (1.0 / CH)
    picked = both[:32] * cos_turns(turns) + both[32:] * cos_turns(turns - 0.25)
    picked = picked * (1.0 / math.sqrt(CH))
    for c in range(4):
        chosen[c] = picked[8 * c : 8 * c + 8].astype(BF16)


def butterflies(wave, halves):
    root = math.sqrt(0.5)

    def one(i, carry):
        rows = pl.ds(pl.multiple_of(16 * i, 16), 16)
        re = [wave[rows, 128 * j : 128 * j + 128].astype(F32) for j in range(8)]
        im = [wave[rows, CH + 128 * j : CH + 128 * j + 128].astype(F32) for j in range(8)]

        def four(ids):
            a, b, c, d = ids
            pr, pi, qr, qi = re[a] + re[c], im[a] + im[c], re[a] - re[c], im[a] - im[c]
            sr, si, tr, ti = re[b] + re[d], im[b] + im[d], re[b] - re[d], im[b] - im[d]
            return [(pr + sr, pi + si), (qr + ti, qi - tr), (pr - sr, pi - si), (qr - ti, qi + tr)]

        even, odd = four((0, 2, 4, 6)), four((1, 3, 5, 7))
        o1 = ((odd[1][0] + odd[1][1]) * root, (odd[1][1] - odd[1][0]) * root)
        o2 = (odd[2][1], -odd[2][0])
        o3 = ((odd[3][1] - odd[3][0]) * root, -(odd[3][0] + odd[3][1]) * root)
        turned = [odd[0], o1, o2, o3]
        for k in range(4):
            for sign in (0, 1):
                zr = even[k][0] - turned[k][0] if sign else even[k][0] + turned[k][0]
                zi = even[k][1] - turned[k][1] if sign else even[k][1] + turned[k][1]
                halves[k + 4 * sign, rows, 0:128] = zr.astype(BF16)
                halves[k + 4 * sign, rows, 128:256] = zi.astype(BF16)
        return carry

    lax.fori_loop(0, 8, one, 0)


def powers(halves, dft, power_k, power):
    def one(k, carry):
        spec = jnp.dot(halves[k], dft[k], preferred_element_type=F32)
        square = spec * spec
        total = square[:, 0:128] + square[:, 128:256]
        mean = total[0:32] + total[32:64] + total[64:96] + total[96:128]
        mean = mean * (1.0 / (FRAMES * CH))
        power_k[:, pl.ds(pl.multiple_of(128 * k, 128), 128)] = mean.astype(BF16)
        return carry

    lax.fori_loop(0, 8, one, 0)
    source = iota((CH, 128), 0)
    target = source // 128 + 8 * (source % 128)

    def put(m, carry):
        select = jnp.where(target == iota((CH, 128), 1) + 128 * m, 1.0, 0.0).astype(BF16)
        block = jnp.dot(power_k[...], select, preferred_element_type=F32)
        power[:, pl.ds(pl.multiple_of(128 * m, 128), 128)] = block.astype(BF16)
        return carry

    lax.fori_loop(0, 8, put, 0)


def stack_weights(raw, rows_f32, weights):
    def one(i, carry):
        lanes = pl.ds(pl.multiple_of(512 * i, 512), 512)
        for k in range(8):
            rows_f32[4 * k : 4 * k + 4, :] = raw[k, :, lanes].astype(F32)
        weights[:, lanes] = rows_f32[...].astype(BF16)
        return carry

    lax.fori_loop(0, 32, one, 0)


def regroup(arrived, x, out):
    lane = iota((8, 128), 1) // E_DEV
    blocks = [arrived[4 * x + c].astype(F32) for c in range(4)]
    frames = []
    for f in range(FRAMES):
        value = None
        for c in range(4):
            shift = ((c - f) % 4) * E_DEV
            moved = pltpu.roll(blocks[c], shift, 1) if shift else blocks[c]
            value = moved if value is None else jnp.where(lane == c, moved, value)
        frames.append(value)
    out[...] = jnp.concatenate(frames, axis=0).astype(BF16)


def kernel(
    volt_h, delay_h, proto_h, map_h, raw_h, dft_h,
    power_h, beams,
    volt, delay_s, map_s, proto_v, taps_a, taps_b, coef, column, basis, wave, chosen, arrived,
    halves, dft, power_k, power, raw, rows_f32, weights, across_a, across_b, total,
    in_sem, volt_sem, out_sem, x_send, x_recv, one_send, one_recv, two_send, two_recv,
):
    z, xl, y = lax.axis_index("z"), lax.axis_index("xl"), lax.axis_index("y")
    xh, core = lax.axis_index("xh"), lax.axis_index("core")
    line = xl * 4 + xh * 2 + core

    def on_line(r):
        other = lax.rem(line + r, LINE)
        return {"xl": other // 4, "xh": lax.rem(other // 2, 2), "core": lax.rem(other, 2)}

    def on_y(r):
        return {"y": lax.rem(y + r, RING)}

    def on_z(r):
        return {"z": lax.rem(z + r, RING)}

    small = [
        pltpu.make_async_copy(delay_h, delay_s, in_sem.at[0]),
        pltpu.make_async_copy(map_h, map_s, in_sem.at[1]),
        pltpu.make_async_copy(proto_h, proto_v, in_sem.at[2]),
    ]
    for copy in small:
        copy.start()
    chunks = []
    for g in range(2):
        for part in range(2):
            rows = pl.ds(16 * g, 16)
            chunks.append(
                pltpu.make_async_copy(volt_h.at[part, rows, :], volt.at[part, rows, :], volt_sem.at[2 * g + part])
            )
    for copy in chunks:
        copy.start()
    later = [
        pltpu.make_async_copy(raw_h, raw, in_sem.at[3]),
        pltpu.make_async_copy(dft_h, dft, in_sem.at[4]),
    ]
    for copy in later:
        copy.start()

    barrier = pltpu.get_barrier_semaphore()
    for r in range(1, LINE):
        pl.semaphore_signal(barrier, inc=1, device_id=on_line(r), device_id_type=MESH)
    for r in range(1, RING):
        pl.semaphore_signal(barrier, inc=1, device_id=on_y(r), device_id_type=MESH)
        pl.semaphore_signal(barrier, inc=1, device_id=on_z(r), device_id_type=MESH)

    for copy in small:
        copy.wait()
    delay_column(delay_s, column)
    rotated_taps(delay_s, proto_v, taps_a, taps_b, coef)
    chosen_basis(map_s, basis)
    for g in range(2):
        for part in range(2):
            chunks[2 * g + part].wait()
            filter_chunk(part, g, volt, coef, column, wave)
    chosen_spectra(delay_s, map_s, basis, wave, chosen)

    pl.semaphore_wait(barrier, LINE - 1 + 2 * (RING - 1))

    x_copies = []
    for r in range(1, LINE):
        other = lax.rem(line + r, LINE)
        copy = pltpu.make_async_remote_copy(
            src_ref=chosen.at[lax.rem(other, 4)],
            dst_ref=arrived.at[line],
            send_sem=x_send.at[r],
            recv_sem=x_recv.at[r],
            device_id=on_line(r),
            device_id_type=MESH,
        )
        copy.start()
        x_copies.append(copy)
    arrived[line] = chosen[lax.rem(line, 4)]

    later[0].wait()
    stack_weights(raw, rows_f32, weights)

    for copy in x_copies:
        copy.wait_recv()
    regroup(arrived, 0, across_a.at[0, 0])
    regroup(arrived, 1, across_b.at[0, 0])

    across = (across_a, across_b)
    first, second = (on_y, on_z), (on_z, on_y)
    ones = {}
    for i in (7, 6, 5, 4, 3, 2, 1):
        r = ORDER[i]
        for colour in range(2):
            copy = pltpu.make_async_remote_copy(
                src_ref=across[colour].at[0, 0],
                dst_ref=across[colour].at[0, r],
                send_sem=one_send.at[colour, r],
                recv_sem=one_recv.at[colour, r],
                device_id=first[colour](r),
                device_id_type=MESH,
            )
            copy.start()
            ones[colour, r] = copy

    later[1].wait()
    butterflies(wave, halves)
    powers(halves, dft, power_k, power)
    power_out = pltpu.make_async_copy(power, power_h, out_sem)
    power_out.start()

    twos = []

    def forward(colour, way, step, i):
        r = ORDER[i]
        held = step if way == 0 else (RING - step) % RING
        given = step + 1 if way == 0 else RING - step - 1
        copy = pltpu.make_async_remote_copy(
            src_ref=across[colour].at[held, r],
            dst_ref=across[colour].at[given, r],
            send_sem=two_send.at[colour, way, step, r],
            recv_sem=two_recv.at[colour, way, step, r],
            device_id=second[colour](1 if way == 0 else RING - 1),
            device_id_type=MESH,
        )
        copy.start()
        twos.append(copy)
        return copy

    def carries(way, step, i):
        if step < 3:
            return True
        return (i % 2 == way) if step == 3 else False

    total[...] = jnp.zeros_like(total)

    def add(pieces):
        data, weight = [], []
        for colour, held, r in pieces:
            zz = lax.rem(z + RING - (held if colour == 0 else r), RING)
            yy = lax.rem(y + RING - (r if colour == 0 else held), RING)
            block = (zz * 2 + colour) * RING + yy
            data.append(across[colour][held, r])
            weight.append(weights[:, pl.ds(pl.multiple_of(block * 128, 128), 128)])
        total[:, 0:32] += nt_dot(jnp.concatenate(data, axis=1), jnp.concatenate(weight, axis=1))

    flying = {}
    for pair in range(4):
        pieces = []
        for i in (2 * pair, 2 * pair + 1):
            for colour in range(2):
                if i:
                    ones[colour, ORDER[i]].wait_recv()
                for way in range(2):
                    flying[colour, way, 0, i] = forward(colour, way, 0, i)
                pieces.append((colour, 0, ORDER[i]))
        add(pieces)
    for step in range(4):
        for pair in range(4):
            pieces = []
            for i in (2 * pair, 2 * pair + 1):
                for colour in range(2):
                    for way in range(2):
                        if not carries(way, step, i):
                            continue
                        flying[colour, way, step, i].wait_recv()
                        if carries(way, step + 1, i):
                            flying[colour, way, step + 1, i] = forward(colour, way, step + 1, i)
                        pieces.append((colour, step + 1 if way == 0 else RING - step - 1, ORDER[i]))
            add(pieces)

    row, col = iota((32, 128), 0), iota((32, 128), 1)
    same = jnp.where((row % 4 == col % 4) & (col < 32), total[...], 0.0)
    folded = same + pltpu.roll(same, 127, 1) + pltpu.roll(same, 126, 1) + pltpu.roll(same, 125, 1)
    wide = folded.reshape(4, 8, 128)
    crossed = pltpu.roll(pltpu.roll(folded, 124, 1).reshape(4, 8, 128), 4, 1)
    real = iota((4, 8, 128), 1) < 4
    beams[...] = jnp.where(real, wide - crossed, wide + crossed).reshape(32, 128)

    for copy in x_copies:
        copy.wait_send()
    for copy in ones.values():
        copy.wait_send()
    for copy in twos:
        copy.wait_send()
    power_out.wait()


def on_device(voltages, delays, prototype, subband_map, beam_weights):
    raw = beam_weights.reshape(8, 4, 16384)
    dft = jnp.asarray(dft_blocks())
    any_spec = pl.BlockSpec(memory_space=pl.ANY)
    dma = pltpu.SemaphoreType.DMA
    power, beams = pl.pallas_call(
        kernel,
        out_shape=(
            jax.ShapeDtypeStruct((E_DEV, CH), BF16),
            jax.ShapeDtypeStruct((32, 128), F32),
        ),
        in_specs=[any_spec] * 6,
        out_specs=(any_spec, pl.BlockSpec(memory_space=pltpu.VMEM)),
        scratch_shapes=[
            pltpu.VMEM((2, E_DEV, SAMP), BF16),
            pltpu.SMEM((E_DEV,), jnp.int32),
            pltpu.SMEM((16,), jnp.int32),
            pltpu.VMEM((TAPS, CH), BF16),
            pltpu.VMEM((128, 128), F32),
            pltpu.VMEM((128, 128), F32),
            pltpu.VMEM((128 * PAD, 128), F32),
            pltpu.VMEM((E_DEV, 128), jnp.int32),
            pltpu.VMEM((64, 2 * CH), BF16),
            pltpu.VMEM((128, 2 * CH), BF16),
            pltpu.VMEM((4, 8, 128), BF16),
            pltpu.VMEM((8, 8, 128), BF16),
            pltpu.VMEM((8, 128, 256), BF16),
            pltpu.VMEM((8, 256, 256), BF16),
            pltpu.VMEM((E_DEV, CH), BF16),
            pltpu.VMEM((E_DEV, CH), BF16),
            pltpu.VMEM((8, 4, 16384), BF16),
            pltpu.VMEM((32, 512), F32),
            pltpu.VMEM((32, 16384), BF16),
            pltpu.VMEM((RING, RING, 32, 128), BF16),
            pltpu.VMEM((RING, RING, 32, 128), BF16),
            pltpu.VMEM((32, 128), F32),
            dma((5,)),
            dma((4,)),
            dma,
            dma((LINE,)),
            dma((LINE,)),
            dma((2, RING)),
            dma((2, RING)),
            dma((2, 2, 4, RING)),
            dma((2, 2, 4, RING)),
        ],
        compiler_params=pltpu.CompilerParams(collective_id=0, has_side_effects=True),
        name="channelize_and_beamform",
    )(voltages, delays, prototype, subband_map, raw, dft)
    beams = beams.reshape(4, 2, 4, 128)[:, :, :, 0:32:8]
    beams = jnp.transpose(beams, (1, 2, 0, 3)).reshape(2, 16, 4)
    return power, beams


def solution(mesh):
    finer = Mesh(mesh.devices.reshape(8, 2, 8, 2, 2), ("z", "xl", "y", "xh", "core"))
    elem, chan = ("z", "xl", "y"), ("xh", "core")
    placed = (P(None, elem + chan, None), P(elem + chan), P(), P(), P(elem, None, chan, None))
    return jax.shard_map(
        on_device,
        mesh=finer,
        in_specs=placed,
        out_specs=(P(elem + chan, None), P(None, chan, elem)),
        check_vma=False,
    )
```

time: 263 us -> 47.1 us (0.18)
  the two profiles are of different devices: /device:TPU:1 before, /device:TPU:8 now
where the time goes in v1:
time: 47.1 us; the launch traced here: 46.8 us
  Pallas kernels  42.3 us (90%)
  local copies, waits for them, and re-layouts  3.92 us (8%)
  between operations  0.64 us (1%)
    pallas_call x1, Pallas kernels, on_device(): pl.pallas_call(kernel, out_shape=(jax.ShapeDtypeStruct((E_DEV, CH), BF16)...  42.3 us
    slice x1, local copies, waits for them, and re-layouts, on_device(): beams = beams.reshape(4, 2, 4, 128)[:, :, :, 0:32:8]  1.62 us
    unnamed x2, local copies, waits for them, and re-layouts  1.61 us

profile of v1, /device:TPU:8, one launch (start us, length us, event | category | flops | bytes accessed | tf_op | source)
XLA Modules:
  0.0 46.8 jit_solution(2155192544514128817)
XLA Ops:
  0.6 42.3 %channelize_and_beamform.1 = (bf16[32,1024]{1,0:T(8,128)(2,1)}, f32[32,128]{1,0:T(8,128)}) custom-call(bf16[2,32,19584]{2,1,0:T(8,128)(2,1)} %volt_h.1, s32[32]{0:T(128)} %delay_h.1, bf16[16,1024]{1,0:T(8,128)(2,1)} %proto_h.1, s32[16]{0:T(128)} %map_h.1, bf16[8,4,16384]{2,1,0:T(4,128)(2,1)} %bitcast.5, bf16[8,256,256]{2,1,0:T(8,128)(2,1)} %constant.2.clone.dft_h), custom_call_target="tpu_custom_call" | custom-call | tf_op jit(solution)/shard_map/channelize_and_beamform/pallas_call | solution.py:429
  42.9 1.6 %slice.3 = f32[4,2,4,4]{3,2,1,0:T(4,128)S(1)} slice(f32[4,2,4,128]{3,2,1,0:T(4,128)} %bitcast.7), slice={[0:4:1], [0:2:1], [0:4:1], [0:32:8]} | slice | bytes 1024 | tf_op jit(solution)/shard_map/slice | solution.py:473
  44.5 0.1 copy.9
  44.7 0.7 %reshape.15 = f32[2,16,4]{1,2,0:T(4,128)} reshape(f32[2,4,4,4]{2,1,3,0:T(4,128)S(1)} %bitcast.6) | data formatting | bytes 1024 | tf_op jit(solution)/shard_map/reshape | solution.py:474
  45.3 1.5 %copy.11 = bf16[32,1024]{1,0:T(8,128)(2,1)} copy(bf16[32,1024]{1,0:T(8,128)(2,1)} %get-tuple-element.8) | data formatting | bytes 131072

commit v2 on v1

--- a/solution.py
+++ b/solution.py
@@ -61,7 +61,7 @@
         coef[pl.ds(n, 128, stride=PAD), :] = pltpu.roll(mixed, d, 1)
         return carry
 
-    lax.fori_loop(0, E_DEV, one, 0)
+    lax.fori_loop(0, E_DEV, one, 0, unroll=8)
 
 
 def delay_column(delay_s, column):
@@ -186,7 +186,7 @@
     lax.fori_loop(0, 8, one, 0)
 
 
-def powers(halves, dft, power_k, power):
+def powers(halves, dft, power_k):
     def one(k, carry):
         spec = jnp.dot(halves[k], dft[k], preferred_element_type=F32)
         square = spec * spec
@@ -197,6 +197,9 @@
         return carry
 
     lax.fori_loop(0, 8, one, 0)
+
+
+def natural_order(power_k, power):
     source = iota((CH, 128), 0)
     target = source // 128 + 8 * (source % 128)
 
@@ -211,18 +214,22 @@
 
 def stack_weights(raw, rows_f32, weights):
     def one(i, carry):
-        lanes = pl.ds(pl.multiple_of(512 * i, 512), 512)
         for k in range(8):
-            rows_f32[4 * k : 4 * k + 4, :] = raw[k, :, lanes].astype(F32)
-        weights[:, lanes] = rows_f32[...].astype(BF16)
+            piece = raw[k, :, pl.ds(pl.multiple_of(512 * i, 512), 512)].astype(F32)
+            for m in range(4):
+                start = 32 * m + 16 * (k % 2) + k // 2
+                rows_f32[pl.ds(start, 4, stride=4), :] = piece[:, 128 * m : 128 * m + 128]
+        for m in range(4):
+            lanes = pl.ds(pl.multiple_of(512 * i + 128 * m, 128), 128)
+            weights[:, lanes] = rows_f32[32 * m : 32 * m + 32, :].astype(BF16)
         return carry
 
     lax.fori_loop(0, 32, one, 0)
 
 
-def regroup(arrived, x, out):
+def regroup(arrived, first, out):
     lane = iota((8, 128), 1) // E_DEV
-    blocks = [arrived[4 * x + c].astype(F32) for c in range(4)]
+    blocks = [arrived[first + c].astype(F32) for c in range(4)]
     frames = []
     for f in range(FRAMES):
         value = None
@@ -234,26 +241,32 @@
     out[...] = jnp.concatenate(frames, axis=0).astype(BF16)
 
 
+def beams_out(total, rows, beams):
+    row, col = iota((32, 128), 0), iota((32, 128), 1)
+    same = jnp.where((row % 4 == (col // 4) % 4) & (col < 32), total[...], 0.0)
+    folded = same + pltpu.roll(same, 124, 1) + pltpu.roll(same, 120, 1) + pltpu.roll(same, 116, 1)
+    wide = folded.reshape(4, 8, 128)
+    crossed = pltpu.roll(pltpu.roll(folded, 112, 1).reshape(4, 8, 128), 4, 1)
+    real = iota((4, 8, 128), 1) < 4
+    rows[...] = jnp.where(real, wide - crossed, wide + crossed).reshape(32, 128)
+    ordered = jnp.concatenate([rows[pl.ds(k, 4, stride=8), :] for k in range(8)], axis=0)
+    turned = ordered.T
+    beams[0] = turned[0:4, 0:16]
+    beams[1] = turned[0:4, 16:32]
+
+
 def kernel(
     volt_h, delay_h, proto_h, map_h, raw_h, dft_h,
     power_h, beams,
     volt, delay_s, map_s, proto_v, taps_a, taps_b, coef, column, basis, wave, chosen, arrived,
-    halves, dft, power_k, power, raw, rows_f32, weights, across_a, across_b, total,
-    in_sem, volt_sem, out_sem, x_send, x_recv, one_send, one_recv, two_send, two_recv,
+    halves, dft, power_k, power, raw, rows_f32, weights, across_a, across_b, total, final,
+    in_sem, volt_sem, out_sem, shot_send, shot_recv, hop_send, hop_recv,
 ):
     z, xl, y = lax.axis_index("z"), lax.axis_index("xl"), lax.axis_index("y")
     xh, core = lax.axis_index("xh"), lax.axis_index("core")
-    line = xl * 4 + xh * 2 + core
-
-    def on_line(r):
-        other = lax.rem(line + r, LINE)
-        return {"xl": other // 4, "xh": lax.rem(other // 2, 2), "core": lax.rem(other, 2)}
-
-    def on_y(r):
-        return {"y": lax.rem(y + r, RING)}
-
-    def on_z(r):
-        return {"z": lax.rem(z + r, RING)}
+    chan = xh * 2 + core
+    ahead_y = [lax.rem(y + r, RING) for r in range(RING)]
+    ahead_z = [lax.rem(z + r, RING) for r in range(RING)]
 
     small = [
         pltpu.make_async_copy(delay_h, delay_s, in_sem.at[0]),
@@ -275,15 +288,26 @@
         pltpu.make_async_copy(raw_h, raw, in_sem.at[3]),
         pltpu.make_async_copy(dft_h, dft, in_sem.at[4]),
     ]
-    for copy in later:
-        copy.start()
 
     barrier = pltpu.get_barrier_semaphore()
-    for r in range(1, LINE):
-        pl.semaphore_signal(barrier, inc=1, device_id=on_line(r), device_id_type=MESH)
-    for r in range(1, RING):
-        pl.semaphore_signal(barrier, inc=1, device_id=on_y(r), device_id_type=MESH)
-        pl.semaphore_signal(barrier, inc=1, device_id=on_z(r), device_id_type=MESH)
+
+    def hello(device):
+        pl.semaphore_signal(barrier, inc=1, device_id=device, device_id_type=MESH)
+
+    others = [lax.rem(chan + q, 4) for q in range(4)]
+    for colour in range(2):
+        for i in range(RING):
+            for q in range(4):
+                device = {"xl": colour, "xh": others[q] // 2, "core": lax.rem(others[q], 2)}
+                device["z" if colour else "y"] = (ahead_z if colour else ahead_y)[i]
+                if i == 0 and q == 0:
+                    pl.when(xl != colour)(functools.partial(hello, device))
+                else:
+                    hello(device)
+    for r in (1, 2, 6, 7):
+        side_y = lax.rem(y + r * xl, RING)
+        side_z = lax.rem(z + r * (1 - xl), RING)
+        hello({"y": side_y, "z": side_z})
 
     for copy in small:
         copy.wait()
@@ -293,131 +317,149 @@
     for g in range(2):
         for part in range(2):
             chunks[2 * g + part].wait()
+            if g == 1 and part == 1:
+                for copy in later:
+                    copy.start()
             filter_chunk(part, g, volt, coef, column, wave)
     chosen_spectra(delay_s, map_s, basis, wave, chosen)
 
-    pl.semaphore_wait(barrier, LINE - 1 + 2 * (RING - 1))
-
-    x_copies = []
-    for r in range(1, LINE):
-        other = lax.rem(line + r, LINE)
-        copy = pltpu.make_async_remote_copy(
-            src_ref=chosen.at[lax.rem(other, 4)],
-            dst_ref=arrived.at[line],
-            send_sem=x_send.at[r],
-            recv_sem=x_recv.at[r],
-            device_id=on_line(r),
+    pl.semaphore_wait(barrier, 2 * RING * 4 - 1 + 4)
+
+    line = xl * 4 + chan
+    mine = xl * 32 + chan
+    places = [lax.rem(line + q, LINE) for q in range(LINE)]
+    for i in range(RING):
+        r = ORDER[i]
+        shot_y = lax.rem(y + r * (1 - xl), RING)
+        shot_z = lax.rem(z + r * xl, RING)
+        for q in (3, 5, 2, 6, 1, 7, 4, 0):
+            if i == 0 and q == 0:
+                continue
+            place = places[q]
+            pltpu.make_async_remote_copy(
+                src_ref=chosen.at[lax.rem(place, 4)],
+                dst_ref=arrived.at[mine + 4 * i],
+                send_sem=shot_send,
+                recv_sem=shot_recv.at[xl * RING + i],
+                device_id={
+                    "xl": place // 4, "xh": lax.rem(place // 2, 2), "core": lax.rem(place, 2),
+                    "y": shot_y, "z": shot_z,
+                },
+                device_id_type=MESH,
+            ).start()
+    arrived[mine] = chosen[chan]
+
+    later[0].wait()
+    stack_weights(raw, rows_f32, weights)
+    butterflies(wave, halves)
+
+    across = (across_a, across_b)
+    aside = ("z", "y")
+    ahead = (ahead_z, ahead_y)
+
+    def shot(colour, i, count):
+        return pltpu.make_async_remote_copy(
+            src_ref=arrived.at[pl.ds(0, count)],
+            dst_ref=arrived.at[pl.ds(colour * 32 + 4 * i, count)],
+            send_sem=shot_send,
+            recv_sem=shot_recv.at[colour * RING + i],
+            device_id={"y": ahead_y[1]},
             device_id_type=MESH,
         )
-        copy.start()
-        x_copies.append(copy)
-    arrived[line] = chosen[lax.rem(line, 4)]
-
-    later[0].wait()
-    stack_weights(raw, rows_f32, weights)
-
-    for copy in x_copies:
-        copy.wait_recv()
-    regroup(arrived, 0, across_a.at[0, 0])
-    regroup(arrived, 1, across_b.at[0, 0])
-
-    across = (across_a, across_b)
-    first, second = (on_y, on_z), (on_z, on_y)
-    ones = {}
-    for i in (7, 6, 5, 4, 3, 2, 1):
-        r = ORDER[i]
+
+    def ready(colour, i):
+        if i:
+            shot(colour, i, 4).wait_recv()
+        else:
+            pl.when(xl == colour)(lambda: shot(colour, i, 3).wait_recv())
+            pl.when(xl != colour)(lambda: shot(colour, i, 4).wait_recv())
+        regroup(arrived, colour * 32 + 4 * i, across[colour].at[0, i])
+
+    def hop(colour, way, kind, i):
+        sign = -1 if way else 1
+        held = (0, 0, 2, 2)[kind] * sign % RING
+        step = (1, 2, 1, 2)[kind] * sign % RING
+        return pltpu.make_async_remote_copy(
+            src_ref=across[colour].at[held, i],
+            dst_ref=across[colour].at[(held + step) % RING, i],
+            send_sem=hop_send.at[colour, way, kind],
+            recv_sem=hop_recv.at[colour, way, kind, i],
+            device_id={aside[colour]: ahead[colour][step]},
+            device_id_type=MESH,
+        )
+
+    total[...] = jnp.zeros_like(total)
+
+    def add(pieces):
+        data, weight = [], []
+        for colour, held, i in pieces:
+            zz = ahead_z[(RING - (held if colour == 0 else ORDER[i])) % RING]
+            yy = ahead_y[(RING - (ORDER[i] if colour == 0 else held)) % RING]
+            block = (zz * 2 + colour) * RING + yy
+            data.append(across[colour][held, i])
+            weight.append(weights[:, pl.ds(pl.multiple_of(block * 128, 128), 128)])
+        total[:, 0:32] += nt_dot(jnp.concatenate(data, axis=1), jnp.concatenate(weight, axis=1))
+
+    for i in range(RING):
         for colour in range(2):
-            copy = pltpu.make_async_remote_copy(
-                src_ref=across[colour].at[0, 0],
-                dst_ref=across[colour].at[0, r],
-                send_sem=one_send.at[colour, r],
-                recv_sem=one_recv.at[colour, r],
-                device_id=first[colour](r),
-                device_id_type=MESH,
-            )
-            copy.start()
-            ones[colour, r] = copy
+            ready(colour, i)
+            for way in range(2):
+                hop(colour, way, 1, i).start()
+                hop(colour, way, 0, i).start()
 
     later[1].wait()
-    butterflies(wave, halves)
-    powers(halves, dft, power_k, power)
+    powers(halves, dft, power_k)
+    pieces = []
+    for i in range(RING):
+        for colour in range(2):
+            for way in range(2):
+                hop(colour, way, 1, i).wait_recv()
+                if i % 2 == way:
+                    hop(colour, way, 3, i).start()
+                hop(colour, way, 2, i).start()
+    natural_order(power_k, power)
     power_out = pltpu.make_async_copy(power, power_h, out_sem)
     power_out.start()
-
-    twos = []
-
-    def forward(colour, way, step, i):
-        r = ORDER[i]
-        held = step if way == 0 else (RING - step) % RING
-        given = step + 1 if way == 0 else RING - step - 1
-        copy = pltpu.make_async_remote_copy(
-            src_ref=across[colour].at[held, r],
-            dst_ref=across[colour].at[given, r],
-            send_sem=two_send.at[colour, way, step, r],
-            recv_sem=two_recv.at[colour, way, step, r],
-            device_id=second[colour](1 if way == 0 else RING - 1),
-            device_id_type=MESH,
-        )
-        copy.start()
-        twos.append(copy)
-        return copy
-
-    def carries(way, step, i):
-        if step < 3:
-            return True
-        return (i % 2 == way) if step == 3 else False
-
-    total[...] = jnp.zeros_like(total)
-
-    def add(pieces):
-        data, weight = [], []
-        for colour, held, r in pieces:
-            zz = lax.rem(z + RING - (held if colour == 0 else r), RING)
-            yy = lax.rem(y + RING - (r if colour == 0 else held), RING)
-            block = (zz * 2 + colour) * RING + yy
-            data.append(across[colour][held, r])
-            weight.append(weights[:, pl.ds(pl.multiple_of(block * 128, 128), 128)])
-        total[:, 0:32] += nt_dot(jnp.concatenate(data, axis=1), jnp.concatenate(weight, axis=1))
-
-    flying = {}
+    add([(colour, 0, i) for colour in range(2) for i in range(RING)])
+    for i in range(RING):
+        for colour in range(2):
+            for way in range(2):
+                hop(colour, way, 0, i).wait_recv()
+    for held in (1, 2, 6, 7):
+        add([(colour, held, i) for colour in range(2) for i in range(RING)])
+    pltpu.make_async_remote_copy(
+        src_ref=arrived.at[pl.ds(0, 63)],
+        dst_ref=arrived.at[pl.ds(0, 63)],
+        send_sem=shot_send,
+        recv_sem=shot_recv.at[0],
+        device_id={"y": ahead_y[1]},
+        device_id_type=MESH,
+    ).wait_send()
     for pair in range(4):
         pieces = []
         for i in (2 * pair, 2 * pair + 1):
             for colour in range(2):
-                if i:
-                    ones[colour, ORDER[i]].wait_recv()
                 for way in range(2):
-                    flying[colour, way, 0, i] = forward(colour, way, 0, i)
-                pieces.append((colour, 0, ORDER[i]))
+                    hop(colour, way, 2, i).wait_recv()
+                    pieces.append((colour, 5 if way else 3, i))
+                    if i % 2 == way:
+                        hop(colour, way, 3, i).wait_recv()
+                        pieces.append((colour, 4, i))
         add(pieces)
-    for step in range(4):
-        for pair in range(4):
-            pieces = []
-            for i in (2 * pair, 2 * pair + 1):
-                for colour in range(2):
-                    for way in range(2):
-                        if not carries(way, step, i):
-                            continue
-                        flying[colour, way, step, i].wait_recv()
-                        if carries(way, step + 1, i):
-                            flying[colour, way, step + 1, i] = forward(colour, way, step + 1, i)
-                        pieces.append((colour, step + 1 if way == 0 else RING - step - 1, ORDER[i]))
-            add(pieces)
-
-    row, col = iota((32, 128), 0), iota((32, 128), 1)
-    same = jnp.where((row % 4 == col % 4) & (col < 32), total[...], 0.0)
-    folded = same + pltpu.roll(same, 127, 1) + pltpu.roll(same, 126, 1) + pltpu.roll(same, 125, 1)
-    wide = folded.reshape(4, 8, 128)
-    crossed = pltpu.roll(pltpu.roll(folded, 124, 1).reshape(4, 8, 128), 4, 1)
-    real = iota((4, 8, 128), 1) < 4
-    beams[...] = jnp.where(real, wide - crossed, wide + crossed).reshape(32, 128)
-
-    for copy in x_copies:
-        copy.wait_send()
-    for copy in ones.values():
-        copy.wait_send()
-    for copy in twos:
-        copy.wait_send()
+    beams_out(total, final, beams)
+
+    for colour in range(2):
+        for way in range(2):
+            for kind in range(4):
+                count = 4 if kind == 3 else 8
+                pltpu.make_async_remote_copy(
+                    src_ref=across[colour].at[0, pl.ds(0, count)],
+                    dst_ref=across[colour].at[0, pl.ds(0, count)],
+                    send_sem=hop_send.at[colour, way, kind],
+                    recv_sem=hop_recv.at[colour, way, kind, 0],
+                    device_id={"y": ahead_y[1]},
+                    device_id_type=MESH,
+                ).wait_send()
     power_out.wait()
 
 
@@ -430,7 +472,7 @@
         kernel,
         out_shape=(
             jax.ShapeDtypeStruct((E_DEV, CH), BF16),
-            jax.ShapeDtypeStruct((32, 128), F32),
+            jax.ShapeDtypeStruct((2, 4, 16), F32),
         ),
         in_specs=[any_spec] * 6,
         out_specs=(any_spec, pl.BlockSpec(memory_space=pltpu.VMEM)),
@@ -446,32 +488,30 @@
             pltpu.VMEM((64, 2 * CH), BF16),
             pltpu.VMEM((128, 2 * CH), BF16),
             pltpu.VMEM((4, 8, 128), BF16),
-            pltpu.VMEM((8, 8, 128), BF16),
+            pltpu.VMEM((64, 8, 128), BF16),
             pltpu.VMEM((8, 128, 256), BF16),
             pltpu.VMEM((8, 256, 256), BF16),
             pltpu.VMEM((E_DEV, CH), BF16),
             pltpu.VMEM((E_DEV, CH), BF16),
             pltpu.VMEM((8, 4, 16384), BF16),
-            pltpu.VMEM((32, 512), F32),
+            pltpu.VMEM((128, 128), F32),
             pltpu.VMEM((32, 16384), BF16),
             pltpu.VMEM((RING, RING, 32, 128), BF16),
             pltpu.VMEM((RING, RING, 32, 128), BF16),
             pltpu.VMEM((32, 128), F32),
+            pltpu.VMEM((32, 128), F32),
             dma((5,)),
             dma((4,)),
             dma,
-            dma((LINE,)),
-            dma((LINE,)),
-            dma((2, RING)),
-            dma((2, RING)),
-            dma((2, 2, 4, RING)),
+            dma,
+            dma((2 * RING,)),
+            dma((2, 2, 4)),
             dma((2, 2, 4, RING)),
         ],
         compiler_params=pltpu.CompilerParams(collective_id=0, has_side_effects=True),
         name="channelize_and_beamform",
     )(voltages, delays, prototype, subband_map, raw, dft)
-    beams = beams.reshape(4, 2, 4, 128)[:, :, :, 0:32:8]
-    beams = jnp.transpose(beams, (1, 2, 0, 3)).reshape(2, 16, 4)
+    beams = jnp.transpose(beams, (0, 2, 1))
     return power, beams
 
 

time: 47.1 us -> 38.4 us (0.82)
  the two profiles are of different devices: /device:TPU:8 before, /device:TPU:1 now
where the time goes in v2:
time: 38.4 us; the launch traced here: 38.2 us
  Pallas kernels  34.8 us (91%)
  local copies, waits for them, and re-layouts  2.74 us (7%)
  between operations  0.64 us (2%)
    pallas_call x1, Pallas kernels, on_device(): pl.pallas_call(kernel, out_shape=(jax.ShapeDtypeStruct((E_DEV, CH), BF16)...  34.8 us
    unnamed x2, local copies, waits for them, and re-layouts  2.74 us

profile of v2, /device:TPU:1, one launch (start us, length us, event | category | flops | bytes accessed | tf_op | source)
XLA Modules:
  0.0 38.2 jit_solution(2224415133060421850)
XLA Ops:
  0.6 34.8 %channelize_and_beamform.1 = (bf16[32,1024]{1,0:T(8,128)(2,1)}, f32[2,4,16]{2,1,0:T(4,128)}) custom-call(bf16[2,32,19584]{2,1,0:T(8,128)(2,1)} %volt_h.1, s32[32]{0:T(128)} %delay_h.1, bf16[16,1024]{1,0:T(8,128)(2,1)} %proto_h.1, s32[16]{0:T(128)} %map_h.1, bf16[8,4,16384]{2,1,0:T(4,128)(2,1)} %bitcast.2, bf16[8,256,256]{2,1,0:T(8,128)(2,1)} %constant.2.clone.dft_h), custom_call_target="tpu_custom_call" | custom-call | tf_op jit(solution)/shard_map/channelize_and_beamform/pallas_call | solution.py:471
  35.4 1.5 %copy.10 = bf16[32,1024]{1,0:T(8,128)(2,1)} copy(bf16[32,1024]{1,0:T(8,128)(2,1)} %get-tuple-element.8) | data formatting | bytes 131072
  36.9 1.3 %copy.11 = f32[2,16,4]{1,2,0:T(4,128)} copy(f32[2,16,4]{1,2,0:T(4,128)} %bitcast.3) | data formatting | bytes 1024

commit v3 on v2

--- a/solution.py
+++ b/solution.py
@@ -61,7 +61,7 @@
         coef[pl.ds(n, 128, stride=PAD), :] = pltpu.roll(mixed, d, 1)
         return carry
 
-    lax.fori_loop(0, E_DEV, one, 0, unroll=8)
+    lax.fori_loop(0, E_DEV, one, 0, unroll=16)
 
 
 def delay_column(delay_s, column):
@@ -82,17 +82,20 @@
 
 
 def chosen_basis(map_s, basis):
-    chan = channel_rows(map_s, 64) * (1.0 / CH)
-    row = iota((64, 128), 0)
-    swapped, second = row // 32, (row // 4) % 2
-    zero = jnp.zeros((64, 128), F32)
-    first_half = jnp.where(swapped == 0, jnp.where(second == 0, zero, 0.25), jnp.where(second == 0, -0.25, zero))
-    last_half = jnp.where(swapped == 0, jnp.where(second == 0, -0.25, zero), jnp.where(second == 0, 0.5 + zero, -0.25))
-    lane = iota((64, 128), 1)
+    chan = channel_rows(map_s, 32) * (1.0 / CH)
+    second = (iota((32, 128), 0) // 4) % 2
+    of_real = jnp.where(second == 0, 0.0, 0.25)
+    of_imag = jnp.where(second == 0, -0.25, 0.0)
+    lane = iota((32, 128), 1)
     for j in range(8):
         turns = chan * (lane + 128 * j).astype(F32)
-        basis[:, 128 * j : 128 * j + 128] = cos_turns(turns + first_half).astype(BF16)
-        basis[:, CH + 128 * j : CH + 128 * j + 128] = cos_turns(turns + last_half).astype(BF16)
+        a = cos_turns(turns + of_real).astype(BF16)
+        b = cos_turns(turns + of_imag).astype(BF16)
+        left, right = slice(128 * j, 128 * j + 128), slice(CH + 128 * j, CH + 128 * j + 128)
+        basis[0:32, left] = a
+        basis[0:32, right] = b
+        basis[32:64, left] = b
+        basis[32:64, right] = -a
 
 
 def filter_block(part, g, j, special, volt, coef, column, wave):
@@ -193,23 +196,21 @@
         total = square[:, 0:128] + square[:, 128:256]
         mean = total[0:32] + total[32:64] + total[64:96] + total[96:128]
         mean = mean * (1.0 / (FRAMES * CH))
-        power_k[:, pl.ds(pl.multiple_of(128 * k, 128), 128)] = mean.astype(BF16)
+        lanes = pl.ds(pl.multiple_of(128 * k, 128), 128)
+        for m in range(8):
+            moved = pltpu.roll(mean, 128 - 16 * m, 1) if m else mean
+            power_k[32 * m : 32 * m + 32, lanes] = moved.astype(BF16)
         return carry
 
-    lax.fori_loop(0, 8, one, 0)
+    lax.fori_loop(0, 8, one, 0, unroll=2)
 
 
 def natural_order(power_k, power):
-    source = iota((CH, 128), 0)
-    target = source // 128 + 8 * (source % 128)
-
-    def put(m, carry):
-        select = jnp.where(target == iota((CH, 128), 1) + 128 * m, 1.0, 0.0).astype(BF16)
-        block = jnp.dot(power_k[...], select, preferred_element_type=F32)
-        power[:, pl.ds(pl.multiple_of(128 * m, 128), 128)] = block.astype(BF16)
-        return carry
-
-    lax.fori_loop(0, 8, put, 0)
+    source, lane = iota((CH, 128), 0), iota((CH, 128), 1)
+    select = jnp.where(lane == source // 128 + 8 * (source % 128), 1.0, 0.0).astype(BF16)
+    ordered = jnp.dot(power_k[...], select, preferred_element_type=F32)
+    for m in range(8):
+        power[:, 128 * m : 128 * m + 128] = ordered[32 * m : 32 * m + 32].astype(BF16)
 
 
 def stack_weights(raw, rows_f32, weights):
@@ -257,10 +258,10 @@
 
 def kernel(
     volt_h, delay_h, proto_h, map_h, raw_h, dft_h,
-    power_h, beams,
+    power, beams,
     volt, delay_s, map_s, proto_v, taps_a, taps_b, coef, column, basis, wave, chosen, arrived,
-    halves, dft, power_k, power, raw, rows_f32, weights, across_a, across_b, total, final,
-    in_sem, volt_sem, out_sem, shot_send, shot_recv, hop_send, hop_recv,
+    halves, dft, power_k, raw, rows_f32, weights, across_a, across_b, total, final,
+    in_sem, volt_sem, shot_send, shot_recv, hop_send, hop_recv,
 ):
     z, xl, y = lax.axis_index("z"), lax.axis_index("xl"), lax.axis_index("y")
     xh, core = lax.axis_index("xh"), lax.axis_index("core")
@@ -352,6 +353,8 @@
     later[0].wait()
     stack_weights(raw, rows_f32, weights)
     butterflies(wave, halves)
+    later[1].wait()
+    powers(halves, dft, power_k)
 
     across = (across_a, across_b)
     aside = ("z", "y")
@@ -407,9 +410,6 @@
                 hop(colour, way, 1, i).start()
                 hop(colour, way, 0, i).start()
 
-    later[1].wait()
-    powers(halves, dft, power_k)
-    pieces = []
     for i in range(RING):
         for colour in range(2):
             for way in range(2):
@@ -418,8 +418,6 @@
                     hop(colour, way, 3, i).start()
                 hop(colour, way, 2, i).start()
     natural_order(power_k, power)
-    power_out = pltpu.make_async_copy(power, power_h, out_sem)
-    power_out.start()
     add([(colour, 0, i) for colour in range(2) for i in range(RING)])
     for i in range(RING):
         for colour in range(2):
@@ -460,12 +458,11 @@
                     device_id={"y": ahead_y[1]},
                     device_id_type=MESH,
                 ).wait_send()
-    power_out.wait()
 
 
 def on_device(voltages, delays, prototype, subband_map, beam_weights):
-    raw = beam_weights.reshape(8, 4, 16384)
-    dft = jnp.asarray(dft_blocks())
+    arrays = (voltages, delays, prototype, subband_map, beam_weights.reshape(8, 4, 16384), jnp.asarray(dft_blocks()))
+    arrays = [pltpu.with_memory_space_constraint(array, pltpu.HBM) for array in arrays]
     any_spec = pl.BlockSpec(memory_space=pl.ANY)
     dma = pltpu.SemaphoreType.DMA
     power, beams = pl.pallas_call(
@@ -475,7 +472,7 @@
             jax.ShapeDtypeStruct((2, 4, 16), F32),
         ),
         in_specs=[any_spec] * 6,
-        out_specs=(any_spec, pl.BlockSpec(memory_space=pltpu.VMEM)),
+        out_specs=(pl.BlockSpec(memory_space=pltpu.VMEM), pl.BlockSpec(memory_space=pltpu.VMEM)),
         scratch_shapes=[
             pltpu.VMEM((2, E_DEV, SAMP), BF16),
             pltpu.SMEM((E_DEV,), jnp.int32),
@@ -491,8 +488,7 @@
             pltpu.VMEM((64, 8, 128), BF16),
             pltpu.VMEM((8, 128, 256), BF16),
             pltpu.VMEM((8, 256, 256), BF16),
-            pltpu.VMEM((E_DEV, CH), BF16),
-            pltpu.VMEM((E_DEV, CH), BF16),
+            pltpu.VMEM((8 * E_DEV, CH), BF16),
             pltpu.VMEM((8, 4, 16384), BF16),
             pltpu.VMEM((128, 128), F32),
             pltpu.VMEM((32, 16384), BF16),
@@ -503,14 +499,13 @@
             dma((5,)),
             dma((4,)),
             dma,
-            dma,
             dma((2 * RING,)),
             dma((2, 2, 4)),
             dma((2, 2, 4, RING)),
         ],
-        compiler_params=pltpu.CompilerParams(collective_id=0, has_side_effects=True),
+        compiler_params=pltpu.CompilerParams(collective_id=0, has_side_effects=True, vmem_limit_bytes=48_000_000),
         name="channelize_and_beamform",
-    )(voltages, delays, prototype, subband_map, raw, dft)
+    )(*arrays)
     beams = jnp.transpose(beams, (0, 2, 1))
     return power, beams
 

time: 38.4 us -> 34.9 us (0.909)
  Pallas kernels: 34.8 us -> 32.8 us
  local copies, waits for them, and re-layouts: 2.74 us -> 1.22 us
    pallas_call x1, Pallas kernels: 34.8 us -> 32.8 us  [on_device(): pl.pallas_call(kernel, out_shape=(jax.ShapeDtypeStruct((E_DEV, CH), BF16)...]
    unnamed x2, local copies, waits for them, and re-layouts: 2.74 us -> 1.22 us
where the time goes in v3:
time: 34.9 us; the launch traced here: 34.7 us
  Pallas kernels  32.8 us (94%)
  local copies, waits for them, and re-layouts  1.22 us (3%)
  between operations  0.64 us (2%)
    pallas_call x1, Pallas kernels, on_device(): pl.pallas_call(kernel, out_shape=(jax.ShapeDtypeStruct((E_DEV, CH), BF16)...  32.8 us
    unnamed x2, local copies, waits for them, and re-layouts  1.22 us

profile of v3, /device:TPU:1, one launch (start us, length us, event | category | flops | bytes accessed | tf_op | source)
XLA Modules:
  0.0 34.7 jit_solution(12053884412465513622)
XLA Ops:
  0.6 32.8 %channelize_and_beamform.1 = (bf16[32,1024]{1,0:T(8,128)(2,1)S(1)}, f32[2,4,16]{2,1,0:T(4,128)S(1)}) custom-call(bf16[2,32,19584]{2,1,0:T(8,128)(2,1)} %volt_h.1, s32[32]{0:T(128)} %delay_h.1, bf16[16,1024]{1,0:T(8,128)(2,1)} %proto_h.1, s32[16]{0:T(128)} %map_h.1, bf16[8,4,16384]{2,1,0:T(4,128)(2,1)} %bitcast.3, bf16[8,256,256]{2,1,0:T(8,128)(2,1)} %constant.2.clone.dft_h), custom_call_target="tpu_custom_call" | custom-call | tf_op jit(solution)/shard_map/channelize_and_beamform/pallas_call | solution.py:468
  33.5 0.6 %copy.10 = bf16[32,1024]{1,0:T(8,128)(2,1)} copy(bf16[32,1024]{1,0:T(8,128)(2,1)S(1)} %get-tuple-element.8) | data formatting | bytes 131072
  34.1 0.6 %copy.11 = f32[2,16,4]{1,2,0:T(4,128)} copy(f32[2,16,4]{1,2,0:T(4,128)S(1)} %bitcast.2) | data formatting | bytes 1024

commit v4 on v3

--- a/solution.py
+++ b/solution.py
@@ -16,7 +16,7 @@
 SAMP = 19584
 RING = 8
 LINE = 8
-PAD = 40
+PAD = 36
 ORDER = (0, 1, 7, 2, 6, 3, 5, 4)
 F32, BF16 = jnp.float32, jnp.bfloat16
 
@@ -122,7 +122,7 @@
         if b < TAPS:
             start = (b * 8 + j) * PAD + 16 * g
             if not isinstance(j, int):
-                start = pl.multiple_of(start, 8)
+                start = pl.multiple_of(start, 4)
             taps[b] = coef[pl.ds(start, 16), :]
         for f in range(FRAMES):
             t = b - f
@@ -283,8 +283,7 @@
             chunks.append(
                 pltpu.make_async_copy(volt_h.at[part, rows, :], volt.at[part, rows, :], volt_sem.at[2 * g + part])
             )
-    for copy in chunks:
-        copy.start()
+    chunks[0].start()
     later = [
         pltpu.make_async_copy(raw_h, raw, in_sem.at[3]),
         pltpu.make_async_copy(dft_h, dft, in_sem.at[4]),
@@ -312,6 +311,8 @@
 
     for copy in small:
         copy.wait()
+    for copy in chunks[1:]:
+        copy.start()
     delay_column(delay_s, column)
     rotated_taps(delay_s, proto_v, taps_a, taps_b, coef)
     chosen_basis(map_s, basis)
@@ -458,6 +459,14 @@
                     device_id={"y": ahead_y[1]},
                     device_id_type=MESH,
                 ).wait_send()
+
+
+def put_out(power, beams, power_h, beams_h, sem):
+    copies = [pltpu.make_async_copy(power, power_h, sem.at[0]), pltpu.make_async_copy(beams, beams_h, sem.at[1])]
+    for copy in copies:
+        copy.start()
+    for copy in copies:
+        copy.wait()
 
 
 def on_device(voltages, delays, prototype, subband_map, beam_weights):
@@ -506,6 +515,15 @@
         compiler_params=pltpu.CompilerParams(collective_id=0, has_side_effects=True, vmem_limit_bytes=48_000_000),
         name="channelize_and_beamform",
     )(*arrays)
+    power, beams = pl.pallas_call(
+        put_out,
+        out_shape=(jax.ShapeDtypeStruct((E_DEV, CH), BF16), jax.ShapeDtypeStruct((2, 4, 16), F32)),
+        in_specs=[pl.BlockSpec(memory_space=pltpu.VMEM)] * 2,
+        out_specs=(pl.BlockSpec(memory_space=pltpu.HBM),) * 2,
+        scratch_shapes=[dma((2,))],
+        compiler_params=pltpu.CompilerParams(vmem_limit_bytes=16_000_000),
+        name="put_out",
+    )(power, beams)
     beams = jnp.transpose(beams, (0, 2, 1))
     return power, beams
 

time: 34.9 us -> 33.6 us (0.963)
  local copies, waits for them, and re-layouts: 1.22 us -> 0 us
    unnamed x2 -> x0, local copies, waits for them, and re-layouts: 1.22 us -> none
    pallas_call x1, Pallas kernels: 32.8 us -> 32.2 us  [on_device(): pl.pallas_call(kernel, out_shape=(jax.ShapeDtypeStruct((E_DEV, CH), BF16)...]
    pallas_call x0 -> x1, Pallas kernels: none -> 0.65 us  [on_device(): pl.pallas_call(put_out, out_shape=(jax.ShapeDtypeStruct((E_DEV, CH), BF16...]
where the time goes in v4:
time: 33.6 us; the launch traced here: 33.5 us
  Pallas kernels  32.8 us (98%)
  between operations  0.64 us (2%)
    pallas_call x1, Pallas kernels, on_device(): pl.pallas_call(kernel, out_shape=(jax.ShapeDtypeStruct((E_DEV, CH), BF16)...  32.2 us

profile of v4, /device:TPU:1, one launch (start us, length us, event | category | flops | bytes accessed | tf_op | source)
XLA Modules:
  0.0 33.5 jit_solution(10595882879219993935)
XLA Ops:
  0.6 32.2 %channelize_and_beamform.1 = (bf16[32,1024]{1,0:T(8,128)(2,1)S(1)}, f32[2,4,16]{2,1,0:T(4,128)S(1)}) custom-call(bf16[2,32,19584]{2,1,0:T(8,128)(2,1)} %volt_h.1, s32[32]{0:T(128)} %delay_h.1, bf16[16,1024]{1,0:T(8,128)(2,1)} %proto_h.1, s32[16]{0:T(128)} %map_h.1, bf16[8,4,16384]{2,1,0:T(4,128)(2,1)} %bitcast.2, bf16[8,256,256]{2,1,0:T(8,128)(2,1)} %constant.2.clone.dft_h), custom_call_target="tpu_custom_call" | custom-call | tf_op jit(solution)/shard_map/channelize_and_beamform/pallas_call | solution.py:477
  32.8 0.7 %put_out.1 = (bf16[32,1024]{1,0:T(8,128)(2,1)}, f32[2,4,16]{2,1,0:T(4,128)}) custom-call(bf16[32,1024]{1,0:T(8,128)(2,1)S(1)} %get-tuple-element.6.power, f32[2,4,16]{2,1,0:T(4,128)S(1)} %get-tuple-element.7.beams), custom_call_target="tpu_custom_call" | custom-call | tf_op jit(solution)/shard_map/put_out/pallas_call | solution.py:518

commit v5 on v4

--- a/solution.py
+++ b/solution.py
@@ -295,16 +295,16 @@
         pl.semaphore_signal(barrier, inc=1, device_id=device, device_id_type=MESH)
 
     others = [lax.rem(chan + q, 4) for q in range(4)]
-    for colour in range(2):
-        for i in range(RING):
-            for q in range(4):
+    for i in range(RING - 1, -1, -1):
+        for colour in range(2):
+            for q in (2, 3, 1, 0):
                 device = {"xl": colour, "xh": others[q] // 2, "core": lax.rem(others[q], 2)}
-                device["z" if colour else "y"] = (ahead_z if colour else ahead_y)[i]
+                device["z" if colour else "y"] = (ahead_z if colour else ahead_y)[ORDER[i]]
                 if i == 0 and q == 0:
                     pl.when(xl != colour)(functools.partial(hello, device))
                 else:
                     hello(device)
-    for r in (1, 2, 6, 7):
+    for r in (2, 6, 1, 7):
         side_y = lax.rem(y + r * xl, RING)
         side_z = lax.rem(z + r * (1 - xl), RING)
         hello({"y": side_y, "z": side_z})
@@ -411,6 +411,15 @@
                 hop(colour, way, 1, i).start()
                 hop(colour, way, 0, i).start()
 
+    def near(pair):
+        pieces = []
+        for i in (2 * pair, 2 * pair + 1):
+            for colour in range(2):
+                for way in range(2):
+                    hop(colour, way, 0, i).wait_recv()
+                pieces += [(colour, held, i) for held in (0, 1, 2, 6, 7)]
+        add(pieces)
+
     for i in range(RING):
         for colour in range(2):
             for way in range(2):
@@ -418,14 +427,9 @@
                 if i % 2 == way:
                     hop(colour, way, 3, i).start()
                 hop(colour, way, 2, i).start()
+        if i % 2:
+            near(i // 2)
     natural_order(power_k, power)
-    add([(colour, 0, i) for colour in range(2) for i in range(RING)])
-    for i in range(RING):
-        for colour in range(2):
-            for way in range(2):
-                hop(colour, way, 0, i).wait_recv()
-    for held in (1, 2, 6, 7):
-        add([(colour, held, i) for colour in range(2) for i in range(RING)])
     pltpu.make_async_remote_copy(
         src_ref=arrived.at[pl.ds(0, 63)],
         dst_ref=arrived.at[pl.ds(0, 63)],

time: 33.6 us -> 33.6 us (level)
  no operation moved by 1% of the time
where the time goes in v5:
time: 33.6 us; the launch traced here: 33.5 us
  Pallas kernels  32.8 us (98%)
  between operations  0.64 us (2%)
    pallas_call x1, Pallas kernels, on_device(): pl.pallas_call(kernel, out_shape=(jax.ShapeDtypeStruct((E_DEV, CH), BF16)...  32.2 us

profile of v5, /device:TPU:1, one launch (start us, length us, event | category | flops | bytes accessed | tf_op | source)
XLA Modules:
  0.0 33.5 jit_solution(10755733122769454876)
XLA Ops:
  0.6 32.2 %channelize_and_beamform.1 = (bf16[32,1024]{1,0:T(8,128)(2,1)S(1)}, f32[2,4,16]{2,1,0:T(4,128)S(1)}) custom-call(bf16[2,32,19584]{2,1,0:T(8,128)(2,1)} %volt_h.1, s32[32]{0:T(128)} %delay_h.1, bf16[16,1024]{1,0:T(8,128)(2,1)} %proto_h.1, s32[16]{0:T(128)} %map_h.1, bf16[8,4,16384]{2,1,0:T(4,128)(2,1)} %bitcast.2, bf16[8,256,256]{2,1,0:T(8,128)(2,1)} %constant.2.clone.dft_h), custom_call_target="tpu_custom_call" | custom-call | tf_op jit(solution)/shard_map/channelize_and_beamform/pallas_call | solution.py:481
  32.8 0.7 %put_out.1 = (bf16[32,1024]{1,0:T(8,128)(2,1)}, f32[2,4,16]{2,1,0:T(4,128)}) custom-call(bf16[32,1024]{1,0:T(8,128)(2,1)S(1)} %get-tuple-element.6.power, f32[2,4,16]{2,1,0:T(4,128)S(1)} %get-tuple-element.7.beams), custom_call_target="tpu_custom_call" | custom-call | tf_op jit(solution)/shard_map/put_out/pallas_call | solution.py:522

commit v6 on v5

--- a/solution.py
+++ b/solution.py
@@ -330,7 +330,7 @@
     line = xl * 4 + chan
     mine = xl * 32 + chan
     places = [lax.rem(line + q, LINE) for q in range(LINE)]
-    for i in range(RING):
+    for i in (7, 0, 1, 2, 3, 4, 5, 6):
         r = ORDER[i]
         shot_y = lax.rem(y + r * (1 - xl), RING)
         shot_z = lax.rem(z + r * xl, RING)

time: 33.6 us -> 34 us (1.012)
  Pallas kernels: 32.8 us -> 33.2 us
    pallas_call x1, Pallas kernels: 32.2 us -> 32.6 us  [on_device(): pl.pallas_call(kernel, out_shape=(jax.ShapeDtypeStruct((E_DEV, CH), BF16)...]
where the time goes in v6:
time: 34 us; the launch traced here: 33.9 us
  Pallas kernels  33.2 us (98%)
  between operations  0.64 us (2%)
    pallas_call x1, Pallas kernels, on_device(): pl.pallas_call(kernel, out_shape=(jax.ShapeDtypeStruct((E_DEV, CH), BF16)...  32.6 us

profile of v6, /device:TPU:1, one launch (start us, length us, event | category | flops | bytes accessed | tf_op | source)
XLA Modules:
  0.0 33.9 jit_solution(9073941798131380380)
XLA Ops:
  0.6 32.6 %channelize_and_beamform.1 = (bf16[32,1024]{1,0:T(8,128)(2,1)S(1)}, f32[2,4,16]{2,1,0:T(4,128)S(1)}) custom-call(bf16[2,32,19584]{2,1,0:T(8,128)(2,1)} %volt_h.1, s32[32]{0:T(128)} %delay_h.1, bf16[16,1024]{1,0:T(8,128)(2,1)} %proto_h.1, s32[16]{0:T(128)} %map_h.1, bf16[8,4,16384]{2,1,0:T(4,128)(2,1)} %bitcast.2, bf16[8,256,256]{2,1,0:T(8,128)(2,1)} %constant.2.clone.dft_h), custom_call_target="tpu_custom_call" | custom-call | tf_op jit(solution)/shard_map/channelize_and_beamform/pallas_call | solution.py:481
  33.2 0.7 %put_out.1 = (bf16[32,1024]{1,0:T(8,128)(2,1)}, f32[2,4,16]{2,1,0:T(4,128)}) custom-call(bf16[32,1024]{1,0:T(8,128)(2,1)S(1)} %get-tuple-element.6.power, f32[2,4,16]{2,1,0:T(4,128)S(1)} %get-tuple-element.7.beams), custom_call_target="tpu_custom_call" | custom-call | tf_op jit(solution)/shard_map/put_out/pallas_call | solution.py:522
